TPU v7x, 768 devices: a whole 4x8x12 slice. The times are simulated.
768 devices in a mesh: enc: 8 (over x, core), row: 24 (over z, y_hi), col: 4 (over y_lo).
Axes of the slice: x: 4, y: 8 (y_hi: 2, y_lo: 4; y = y_hi * 4 + y_lo), z: 12, core: 2. Of those that a mesh axis runs over, the one named last changes fastest.
Arguments:
- out_grad: bfloat16 [288, 8192], P(None, ('enc', 'col')), may hold values from -6 to 6
- gate_pre: bfloat16 [288, 29568], P('enc', 'row'), may hold values from -6 to 6
- up_pre: bfloat16 [288, 29568], P('enc', 'row'), may hold values from -6 to 6
- w_gate: bfloat16 [8192, 29568], P(('enc', 'col'), 'row'), may hold values from -0.0625 to 0.0625
- w_up: bfloat16 [8192, 29568], P(('enc', 'col'), 'row'), may hold values from -0.0625 to 0.0625
- w_down: bfloat16 [29568, 8192], P('row', ('enc', 'col')), may hold values from -0.03125 to 0.03125
- w_proj: bfloat16 [12800, 8192], P(None, ('enc', 'col')), may hold values from -0.0546875 to 0.0546875
- enc_hidden: bfloat16 [1152, 6400], P('row', ('enc', 'col')), may hold values from -6 to 6
- route: int32 [288], replicated, may hold values from 0 to 287, each once
- img_count: int32 [24], replicated, may hold values from 1 to 12
Outputs:
- enc_grad: bfloat16 [3200, 6400], P(None, ('enc', 'col'))
Inputs may be any that keep to these rules, and one draw needn't show every extreme that they name: route[12 * r + k] is the language row that holds slot k of row group r; every language row appears once. Slots k of row group r with k >= img_count[r] are empty.
All inputs are finite; a program needn't handle non-finite values.
Results may differ from a plain program's by a relative error of at most 0.02.
Values may be sent and summed in bfloat16 or wider, within the bound.
A program may use at most 64 MiB of HBM per device.

v0:
```python
import math

import jax
import jax.numpy as jnp
from jax import lax
from jax.sharding import PartitionSpec as P

SHUF = 4
IMG = 12


def split_up(x, dim, size):
    before, after = (x.shape[:dim], x.shape[dim + 1 :])
    return jnp.moveaxis(x.reshape(*before, size, -1, *after), dim, 0)


def summed_on_arrival(x, axis, dim):
    size = lax.axis_size(axis)
    parts = lax.all_to_all(split_up(x, dim, size), axis, 0, 0, tiled=True)
    return jnp.sum(parts, axis=0)


def sent_together(arrays, axis, dim, along):
    ends, at = ([], 0)
    for a in arrays[:-1]:
        at += a.shape[along]
        ends.append(at)
    both = jnp.concatenate(arrays, axis=along)
    return tuple(jnp.split(lax.all_gather(both, axis, axis=dim, tiled=True), ends, axis=along))


def sent_to_all(x, axis):
    copies = jnp.broadcast_to(x, (lax.axis_size(axis), *x.shape))
    return lax.all_to_all(copies, axis, split_axis=0, concat_axis=0, tiled=True)


def in_order(parts, dim):
    lengths = list(parts.shape[1:])
    lengths[dim] *= parts.shape[0]
    return jnp.moveaxis(parts, 0, dim).reshape(lengths)


def gather_directly(x, axis, dim):
    parts = sent_to_all(x, axis)
    return in_order(parts, dim)


def contract_last(left, right):
    return lax.dot_general(
        left, right, (((1,), (1,)), ((), ())), preferred_element_type=jnp.float32
    )


def contract_first(left, right):
    return lax.dot_general(
        left, right, (((0,), (0,)), ((), ())), preferred_element_type=jnp.float32
    )


def gate_grads(hidden_grad, gate_pre, up_pre):
    share_rows = hidden_grad.shape[0]
    offset = lax.axis_index("col") * share_rows
    gate_vals = lax.dynamic_slice_in_dim(gate_pre, offset, share_rows, 0).astype(jnp.float32)
    up_vals = lax.dynamic_slice_in_dim(up_pre, offset, share_rows, 0).astype(jnp.float32)
    squash = jax.nn.sigmoid(gate_vals)
    grad_gate = (hidden_grad * up_vals * squash * (1.0 + gate_vals * (1.0 - squash))).astype(
        jnp.bfloat16
    )
    grad_up = (hidden_grad * gate_vals * squash).astype(jnp.bfloat16)
    return (grad_gate, grad_up)


def shards(out_grad, gate_pre, up_pre, w_gate, w_up, w_down, w_proj, enc_hidden, route, img_count):
    hidden_part = contract_last(out_grad, w_down)
    enc_share = summed_on_arrival(hidden_part, "enc", 0)
    hidden_grad = summed_on_arrival(enc_share, "col", 0)
    grad_gate, grad_up = gate_grads(hidden_grad, gate_pre, up_pre)
    grad_gate, grad_up = sent_together((grad_gate, grad_up), "col", 0, 1)
    grad_gate, grad_up = sent_together((grad_gate, grad_up), "enc", 0, 1)
    routed_gate = jnp.take(grad_gate, route, axis=0)
    routed_up = jnp.take(grad_up, route, axis=0)
    input_part = contract_last(routed_gate, w_gate) + contract_last(routed_up, w_up)
    positions = jnp.arange(route.shape[0], dtype=jnp.int32)
    alive_mask = positions % IMG < jnp.repeat(img_count, IMG)
    input_part = jnp.where(alive_mask[:, None], input_part, jnp.zeros_like(input_part))
    image_grad = summed_on_arrival(input_part, "row", 0).astype(jnp.bfloat16)
    shuffled_grad = summed_on_arrival(contract_last(image_grad, w_proj), ("enc", "col"), 1)
    feature_share = shuffled_grad.shape[1] // SHUF
    patch_grad = (
        shuffled_grad.reshape(IMG, feature_share, SHUF)
        .transpose(0, 2, 1)
        .reshape(IMG * SHUF, feature_share)
        .astype(jnp.bfloat16)
    )
    patch_total = enc_hidden.shape[0] * lax.axis_size("row")
    scale = 1.0 / math.sqrt(patch_total)
    group_term = contract_first(gather_directly(patch_grad, ("enc", "col"), 1), enc_hidden) * scale
    total = lax.psum(group_term.astype(jnp.bfloat16), "row")
    return total


def solution(mesh):
    placed = (
        P(None, ("enc", "col")),
        P("enc", "row"),
        P("enc", "row"),
        P(("enc", "col"), "row"),
        P(("enc", "col"), "row"),
        P("row", ("enc", "col")),
        P(None, ("enc", "col")),
        P("row", ("enc", "col")),
        P(),
        P(),
    )
    return jax.shard_map(
        shards, mesh=mesh, in_specs=placed, out_specs=P(None, ("enc", "col")), check_vma=False
    )
```

profile of v0, /device:TPU:6, one launch (start us, length us, event | category | flops | bytes accessed | tf_op | source)
XLA Modules:
  0.0 517.9 jit_solution(93391914772940740)
XLA Ops:
  6.5 1.1 copy-done
  7.6 2.4 fusion.26
  10.0 1.4 reshape.42
  11.5 32.8 %all_to_all.25 = f32[8,36,1232]{2,1,0:T(8,128)} all-to-all(f32[8,36,1232]{2,1,0:T(8,128)S(1)} %reshape.42), channel_id=1, replica_groups=mesh['enc'=8,'row'=24,'col'=4] {'enc'}, dimensions={0} | all-to-all | bytes 2838528 | tf_op jit(solution)/shard_map/all_to_all | solution.py:19
  44.3 1.5 reduce_sum.36
  45.9 0.8 reshape.43
  46.6 3.5 all-to-all-start.1
  50.1 10.4 %all-to-all-done.1 = f32[4,9,1232]{2,1,0:T(8,128)S(1)} async-done(((f32[4,9,1232]{2,1,0:T(8,128)}), f32[4,9,1232]{2,1,0:T(8,128)S(1)}, u32[]{:S(2)}, u32[]{:S(2)}) %all-to-all-start.1) | async-done | bytes 177440 | tf_op jit(solution)/shard_map/all_to_all | solution.py:19
  60.6 0.9 fusion.14
  61.6 14.7 %all-gather = bf16[4,9,2464]{2,1,0:T(8,128)(2,1)S(1)} all-gather(bf16[1,9,2464]{2,1,0:T(8,128)(2,1)S(1)} %maximum_bitcast_fusion), channel_id=1, replica_groups=mesh['enc'=8,'row'=24,'col'=4] {'col'}, dimensions={0}, use_global_device_ids=true | all-gather | bytes 221760 | tf_op jit(solution)/shard_map/all_gather | solution.py:29
  76.3 0.8 reshape.67
  77.4 29.7 %all-gather.4.cloned.1.call-done = bf16[8,36,2464]{2,1,0:T(8,128)(2,1)} async-done(((bf16[1,36,2464]{2,1,0:T(8,128)(2,1)}), bf16[8,36,2464]{2,1,0:T(8,128)(2,1)}) %all-gather.4.cloned.1.call-update) | async-done | bytes 1419280 | tf_op jit(solution)/shard_map/all_gather | solution.py:29
  107.0 2.6 reshape.68
  109.7 1.7 fusion.25
  111.4 2.2 gather_fusion
  113.6 2.2 gather_fusion.1
  117.3 38.8 %all_to_all.26 = f32[24,12,256]{2,1,0:T(8,128)S(1)} all-to-all(f32[24,12,256]{2,1,0:T(8,128)S(1)} %reshape.44), channel_id=1, replica_groups=mesh['enc'=8,'row'=24,'col'=4] {'row'}, dimensions={0} | all-to-all | bytes 589824 | tf_op jit(solution)/shard_map/all_to_all | solution.py:19
  156.1 4.7 fusion.27
  160.8 0.8 reshape.45
  162.0 30.1 %all_to_all.27 = f32[32,12,400]{2,1,0:T(8,128)S(1)} all-to-all(f32[32,12,400]{2,1,0:T(8,128)S(1)} %bitcast.18), channel_id=1, replica_groups=mesh['enc'=8,'row'=24,'col'=4] {'enc','col'}, dimensions={0} | all-to-all | bytes 1228800 | tf_op jit(solution)/shard_map/all_to_all | solution.py:19
  192.5 18.3 %all_to_all.28 = bf16[32,48,100]{2,1,0:T(8,128)(2,1)S(1)} all-to-all(bf16[32,48,100]{2,1,0:T(8,128)(2,1)S(1)} %broadcast_in_dim.30), channel_id=1, replica_groups=mesh['enc'=8,'row'=24,'col'=4] {'enc','col'}, dimensions={0} | all-to-all | bytes 614400 | tf_op jit(solution)/shard_map/all_to_all | solution.py:34
  211.5 1.6 fusion
  213.1 295.5 %all-reduce.2.cloned.1.call-done = bf16[3200,200]{0,1:T(8,128)(2,1)} async-done(((bf16[3200,200]{0,1:T(8,128)(2,1)}), bf16[3200,200]{0,1:T(8,128)(2,1)}) %all-reduce.2.cloned.1.call-update) | async-done | bytes 1280016 | tf_op jit(solution)/shard_map/psum | solution.py:98
  508.6 2.4 copy.21
  (33 shorter events, 3.5 us)
Async XLA Ops:
  6.5 1.1 copy-start
  45.8 31.3 %copy-start.3 = (s32[24]{0:T(128)S(1)}, s32[24]{0:T(128)}, u32[]{:S(2)}) copy-start(s32[24]{0:T(128)} %param.21) | copy-start | bytes 292
  45.9 31.5 %copy-start.2 = (s32[288]{0:T(512)S(1)}, s32[288]{0:T(512)}, u32[]{:S(2)}) copy-start(s32[288]{0:T(512)} %param.20) | copy-start | bytes 3460
  46.6 14.0 %all-to-all-start.1 = ((f32[4,9,1232]{2,1,0:T(8,128)}), f32[4,9,1232]{2,1,0:T(8,128)S(1)}, u32[]{:S(2)}, u32[]{:S(2)}) async-start(f32[4,9,1232]{2,1,0:T(8,128)} %reshape.43), calls=%async_computation.1 | async-start | bytes 655360 | tf_op jit(solution)/shard_map/all_to_all | solution.py:19
  50.1 57.0 %all-gather.4.cloned.1.call-start = ((), (), s32[]{:S(2)}) async-start(), calls=%async_computation.6 | async-start | bytes 1843200 | tf_op jit(solution)/shard_map/all_gather | solution.py:29
  77.1 431.5 %all-reduce.2.cloned.1.call-start = ((), (), s32[]{:S(2)}) async-start(), calls=%async_computation.5 | async-start | bytes 2560000 | tf_op jit(solution)/shard_map/psum | solution.py:98
  113.5 2.2 copy-start.4
  115.7 1.1 copy-start.5
  192.2 19.3 %copy-start.1 = (bf16[48,200]{1,0:T(8,128)(2,1)S(1)}, bf16[48,200]{1,0:T(8,128)(2,1)}, u32[]{:S(2)}) copy-start(bf16[48,200]{1,0:T(8,128)(2,1)} %param.19) | copy-start | bytes 57604
Sparse Core Ops, SparseCore 0:
  77.2 29.7 all-gather.3
  213.2 295.3 all-reduce.1
where the time goes:
time: 519 us; the launch traced here: 518 us
  waiting for transfers between devices  336 us (65%)
  blocking collectives  135 us (26%)
  local copies, waits for them, and re-layouts  18.2 us (4%)
  between operations  13.6 us (3%)
  matrix products  9.51 us (2%)
    psum x1, waiting for transfers between devices, shards(): total = lax.psum(group_term.astype(jnp.bfloat16), 'row')  295 us
    all_to_all x3, blocking collectives, summed_on_arrival(): parts = lax.all_to_all(split_up(x, dim, size), axis, 0, 0, tiled=True)  102 us
    all_gather x1, waiting for transfers between devices, sent_together(): lax.all_gather(both, axis, axis=dim, tiled=True)  29.7 us
    all_to_all x1, blocking collectives, sent_to_all(): return lax.all_to_all(copies, axis, split_axis=0, concat_axis=0, tiled=True)  18.3 us
    all_gather x1, blocking collectives, sent_together(): lax.all_gather(both, axis, axis=dim, tiled=True)  14.7 us
    all_to_all x1, waiting for transfers between devices, summed_on_arrival(): parts = lax.all_to_all(split_up(x, dim, size), axis, 0, 0, tiled=True)  10.4 us
  transfers between devices with their start and end apart: 3, of which 3 were waited for; matrix products, arithmetic and copies ran while one was open for 0% of the time, Pallas kernels for 0%

commit v1 on v0

v1 whole, which is shorter than its diff:
```python
import functools
import math

import jax
import jax.numpy as jnp
from jax import lax
from jax.experimental import pallas as pl
from jax.experimental.pallas import tpu as pltpu
from jax.sharding import PartitionSpec as P

F32 = jnp.float32
BF16 = jnp.bfloat16
MESH = pl.DeviceIdType.MESH

NI = 288
ROWT = NI // 16
KD = 256
HID = 1232
HIDP = 1280
LT = HIDP // 128
GR = 36
GRP = 80
EC = 200
HT = 192
YT = 96
IMG = 12
PATCH = 1152
FT = 128
PIECE = 224
LAG = 2


def dot_nt(a, b):
    return lax.dot_general(a, b, (((1,), (1,)), ((), ())), preferred_element_type=F32)


def dot_nn(a, b):
    return lax.dot_general(a, b, (((1,), (0,)), ((), ())), preferred_element_type=F32)


def iota(shape, dim):
    return lax.broadcasted_iota(jnp.int32, shape, dim)


def onehot(pred):
    return jnp.where(pred, jnp.float32(1), jnp.float32(0)).astype(BF16)


def await_bytes(ref, sem):
    pltpu.make_async_copy(ref, ref, sem).wait()


def kernel(
    og_h, g_h, u_h, wg_h, wu_h, wd_h, wp_h, eh_h, rt, cnt, out,
    og, wd, wg, wu, wpm, wpp, graw, uraw, eraw, gpad, upad,
    gu, ebuf, hbuf, ra1, s1, ra2, s2, ra3, hfull, fa, fb,
    xb, rb1, sb, rb2, xfull, ept,
    yb, rc1, c1, rc2, c2, yfull, fin,
    lsem, ssem, rsem,
):
    e, r, c = lax.axis_index("enc"), lax.axis_index("row"), lax.axis_index("col")
    x, core = e // 2, e % 2
    z, yh = r // 2, r % 2

    sib = (x * 2 + (1 - core), r, c)
    other_y = (e, z * 2 + (1 - yh), c)

    def at_x(k):
        return lax.rem(x + k, 4)

    def at_c(k):
        return lax.rem(c + k, 4)

    def at_z(k):
        return lax.rem(z + k, 12)

    def dev_x(k):
        return (at_x(k) * 2 + core, r, c)

    def dev_c(k):
        return (e, r, at_c(k))

    def dev_z(k):
        return (e, at_z(k) * 2 + yh, c)

    def send(src, dst, n, to):
        pltpu.make_async_remote_copy(
            src_ref=src, dst_ref=dst, send_sem=ssem.at[n], recv_sem=rsem.at[n],
            device_id=to, device_id_type=MESH,
        ).start()

    def local(src, dst, n):
        copy = pltpu.make_async_copy(src, dst, lsem.at[n])
        copy.start()
        return copy

    wp_main = wp_h.at[pl.ds(pl.multiple_of(r * 512, 512), 512)]
    wp_tail = wp_h.at[pl.ds(pl.multiple_of(12288 + 32 * jnp.minimum(r, 15), 32), 32)]
    load_og = local(og_h, og, 0)
    load_wd = local(wd_h, wd.at[pl.ds(0, HID)], 1)
    load_g = local(g_h, graw, 2)
    load_u = local(u_h, uraw, 3)
    load_e = local(eh_h, eraw, 4)
    load_wg = local(wg_h, wg.at[pl.ds(0, HID)], 5)
    load_wu = local(wu_h, wu.at[pl.ds(0, HID)], 6)
    load_wm = local(wp_main, wpm.at[pl.ds(0, 512)], 7)
    load_wt = local(wp_tail, wpm.at[pl.ds(512, 32)], 8)

    barrier = pltpu.get_barrier_semaphore()
    pl.semaphore_signal(barrier, inc=1, device_id=sib, device_id_type=MESH)
    pl.semaphore_signal(barrier, inc=1, device_id=other_y, device_id_type=MESH)
    for k in range(1, 4):
        pl.semaphore_signal(barrier, inc=1, device_id=dev_x(k), device_id_type=MESH)
        pl.semaphore_signal(barrier, inc=1, device_id=dev_c(k), device_id_type=MESH)
    for k in range(1, 12):
        pl.semaphore_signal(barrier, inc=1, device_id=dev_z(k), device_id_type=MESH)

    tail = jnp.zeros((HIDP - HID, KD), BF16)
    wd[HID:, :] = tail
    wg[HID:, :] = tail
    wu[HID:, :] = tail
    gpad[...] = jnp.zeros_like(gpad)
    upad[...] = jnp.zeros_like(upad)
    hbuf[ROWT * LT :] = jnp.zeros((HT - ROWT * LT, 16, 128), BF16)
    yb[ROWT * 5 :] = jnp.zeros((YT - ROWT * 5, 16, 128), BF16)
    ebuf[r] = jnp.zeros((48, 256), BF16)

    load_g.wait()
    load_u.wait()
    gpad[0:GR, 0:HID] = graw[...]
    upad[0:GR, 0:HID] = uraw[...]
    row, lane = iota((GRP, 48), 0), iota((GRP, 48), 1)
    pick_g = onehot((row == lane) & (lane < GR))
    pick_u = onehot((row == lane + GR) & (lane < GR))
    stacked = dot_nn(pick_g, gpad[...]) + dot_nn(pick_u, upad[...])
    stacked = stacked.astype(BF16)
    gu[0, x, core] = stacked[:, 0:640]
    gu[1, x, core] = stacked[:, 640:1280]
    load_e.wait()
    ebuf[r, :, 0:EC] = eraw[...]

    load_og.wait()
    load_wd.wait()

    def hidden(j, carry):
        w = wd[pl.ds(pl.multiple_of(j * 128, 128), 128), :]
        part = dot_nt(og[...], w)
        hbuf[pl.ds(j * ROWT, ROWT)] = part.reshape(ROWT, 16, 128).astype(BF16)
        return carry

    lax.fori_loop(0, LT, hidden, 0)

    pl.semaphore_wait(barrier, 19)

    half = HT // 2
    send(hbuf.at[pl.ds((1 - core) * half, half)], ra1, 0, sib)
    for k in range(1, 4):
        send(gu.at[0, x, core], gu.at[0, x, core], 10, dev_x(k))
    send(ebuf.at[r], ebuf.at[r], 12, other_y)
    await_bytes(ra1, rsem.at[0])
    mine = hbuf[pl.ds(core * half, half)].astype(F32) + ra1[...].astype(F32)
    s1[...] = mine.astype(BF16).reshape(4, 24, 16, 128)

    for k in range(1, 4):
        send(s1.at[at_x(k)], ra2.at[k - 1], 1, dev_x(k))
    for k in range(1, 4):
        send(gu.at[1, x, core], gu.at[1, x, core], 11, dev_x(k))
    await_bytes(ebuf.at[0], rsem.at[12])
    await_bytes(ebuf.at[0], ssem.at[12])
    pair = ebuf.at[pl.ds(2 * z, 2)]
    for k in range(1, 12):
        send(pair, pair, 13, dev_z(k))
    await_bytes(ra2, rsem.at[1])
    got = s1[x].astype(F32)
    for k in range(3):
        got = got + ra2[k].astype(F32)
    s2[...] = got.astype(BF16).reshape(4, 6, 16, 128)

    for k in range(1, 4):
        send(s2.at[at_c(k)], ra3.at[k - 1], 2, dev_c(k))

    load_wm.wait()
    load_wt.wait()
    for q in range(4):
        move = onehot(iota((128, 512), 1) == 4 * iota((128, 512), 0) + q)
        wpp[q * 128 : (q + 1) * 128, :] = dot_nn(move, wpm[0:512, :]).astype(BF16)
    row, lane = iota((128, 32), 0), iota((128, 32), 1)
    move = onehot((lane == 4 * (row & 7) + (row >> 3)) & (row < 32))
    wpp[512:640, :] = dot_nn(move, wpm[512:544, :]).astype(BF16)

    await_bytes(ra3, rsem.at[2])
    got = s2[c].astype(F32)
    for k in range(3):
        got = got + ra3[k].astype(F32)
    base = core * half + x * 24
    hfull[pl.ds(base + c * 6, 6)] = got.astype(BF16)

    own = hfull.at[pl.ds(base + c * 6, 6)]
    for k in range(1, 4):
        send(own, own, 3, dev_c(k))
    await_bytes(gu.at[0, pl.ds(0, 3), 0], rsem.at[10])
    await_bytes(gu.at[0, pl.ds(0, 3), 0], rsem.at[11])
    await_bytes(gu.at[0, pl.ds(0, 3), 0], ssem.at[10])
    await_bytes(gu.at[0, pl.ds(0, 3), 0], ssem.at[11])
    send(gu.at[:, :, core], gu.at[:, :, core], 14, sib)
    await_bytes(hfull.at[pl.ds(0, 18)], rsem.at[3])
    await_bytes(hfull.at[pl.ds(0, 18)], ssem.at[3])
    own = hfull.at[pl.ds(base, 24)]
    for k in range(1, 4):
        send(own, own, 4, dev_x(k))

    await_bytes(gu.at[:, :, 0], rsem.at[14])
    await_bytes(gu.at[:, :, 0], ssem.at[14])
    col = iota((NI, 8 * GRP), 1)
    target = col
    for s in range(1, 8):
        target = target - jnp.where(col >= GRP * s, GRP - GR, 0)
    start_of = jnp.zeros_like(col)
    for s in range(1, 8):
        start_of = start_of + jnp.where(col >= GRP * s, GRP, 0)
    within = col - start_of
    row = iota((NI, 8 * GRP), 0)
    place_g = onehot((row == target) & (within < GR))
    place_u = onehot((row == target - GR) & (within >= GR) & (within < 2 * GR))

    for h in range(2):
        def factors(j, carry):
            rows = gu[h, :, :, :, pl.ds(pl.multiple_of(j * 128, 128), 128)]
            rows = rows.reshape(8 * GRP, 128)
            gate = dot_nn(place_g, rows)
            up = dot_nn(place_u, rows)
            squash = 1.0 / (1.0 + jnp.exp(-gate))
            fa[h * 5 + j] = up * squash * (1.0 + gate * (1.0 - squash))
            fb[h * 5 + j] = gate * squash
            return carry

        lax.fori_loop(0, 5, factors, 0)

    await_bytes(hfull.at[pl.ds(0, 72)], rsem.at[4])
    await_bytes(hfull.at[pl.ds(0, 72)], ssem.at[4])
    own = hfull.at[pl.ds(core * half, half)]
    send(own, own, 5, sib)
    load_wg.wait()
    load_wu.wait()
    await_bytes(hfull.at[pl.ds(0, half)], rsem.at[5])
    await_bytes(hfull.at[pl.ds(0, half)], ssem.at[5])

    def inputs(j, total):
        h = hfull[pl.ds(j * ROWT, ROWT)].astype(F32).reshape(NI, 128)
        cut = pl.ds(pl.multiple_of(j * 128, 128), 128)
        total = total + dot_nn((h * fa[j]).astype(BF16), wg[cut, :])
        return total + dot_nn((h * fb[j]).astype(BF16), wu[cut, :])

    part = lax.fori_loop(0, LT, inputs, jnp.zeros((NI, KD), F32))
    for l in range(2):
        xb[l * 36 : (l + 1) * 36] = part[:, l * 128 : (l + 1) * 128].reshape(36, 8, 128).astype(BF16)

    for k in range(1, 12):
        send(xb.at[pl.ds(at_z(k) * 6, 6)], rb1.at[k - 1], 6, dev_z(k))

    await_bytes(ebuf.at[pl.ds(0, 22)], rsem.at[13])
    await_bytes(ebuf.at[pl.ds(0, 22)], ssem.at[13])
    lane = iota((1, NI), 1)
    limit = jnp.zeros((1, NI), jnp.int32)
    for s in range(24):
        inside = (lane >= s * IMG) & (lane < (s + 1) * IMG)
        limit = jnp.where(inside, s * IMG + cnt[s], limit)
    slot_row = jnp.where(lane < limit, rt[...], -1)
    routed = onehot(iota((NI, NI), 0) == slot_row)
    et = ebuf[...].reshape(PATCH, 256).astype(F32).T.astype(BF16)
    for q in range(4):
        take = onehot(iota((PATCH, NI), 0) == 4 * iota((PATCH, NI), 1) + q)
        plane = dot_nn(et, take).astype(BF16)
        ept[q] = dot_nt(plane, routed).astype(BF16)

    await_bytes(rb1, rsem.at[6])
    got = xb[pl.ds(z * 6, 6)].astype(F32)
    for k in range(11):
        got = got + rb1[k].astype(F32)
    sb[...] = got.astype(BF16)
    send(sb, rb2, 7, other_y)
    await_bytes(rb2, rsem.at[7])
    xfull[pl.ds(z * 6, 6)] = (sb[...].astype(F32) + rb2[...].astype(F32)).astype(BF16)
    own = xfull.at[pl.ds(z * 6, 6)]
    for k in range(1, 12):
        send(own, own, 8, dev_z(k))
    await_bytes(xfull.at[pl.ds(0, 66)], rsem.at[8])
    await_bytes(xfull.at[pl.ds(0, 66)], ssem.at[8])

    both = xfull[...].astype(F32)
    left = both[0:36].reshape(NI, 128).astype(BF16)
    right = both[36:72].reshape(NI, 128).astype(BF16)
    for q in range(5):
        w = wpp[q * 128 : (q + 1) * 128, :]
        part = dot_nt(left, w[:, 0:128]) + dot_nt(right, w[:, 128:256])
        yb[q * ROWT : (q + 1) * ROWT] = part.reshape(ROWT, 16, 128).astype(BF16)

    half = YT // 2
    send(yb.at[pl.ds((1 - core) * half, half)], rc1, 9, sib)
    await_bytes(rc1, rsem.at[9])
    mine = yb[pl.ds(core * half, half)].astype(F32) + rc1[...].astype(F32)
    c1[...] = mine.astype(BF16).reshape(4, 12, 16, 128)
    for k in range(1, 4):
        send(c1.at[at_x(k)], rc2.at[k - 1], 15, dev_x(k))
    await_bytes(rc2, rsem.at[15])
    got = c1[x].astype(F32)
    for k in range(3):
        got = got + rc2[k].astype(F32)
    c2[c] = got.astype(BF16)
    for k in range(1, 4):
        send(c2.at[c], c2.at[c], 16, dev_c(k))
    await_bytes(c2.at[pl.ds(0, 3)], rsem.at[16])
    got = c2[0].astype(F32)
    for k in range(1, 4):
        got = got + c2[k].astype(F32)
    base = core * half + x * 12
    yfull[pl.ds(base, 12)] = got.astype(BF16)
    own = yfull.at[pl.ds(base, 12)]
    for k in range(1, 4):
        send(own, own, 17, dev_x(k))
    await_bytes(yfull.at[pl.ds(0, 36)], rsem.at[17])
    await_bytes(yfull.at[pl.ds(0, 36)], ssem.at[17])
    own = yfull.at[pl.ds(core * half, half)]
    send(own, own, 18, sib)
    await_bytes(yfull.at[pl.ds(0, half)], rsem.at[18])
    await_bytes(yfull.at[pl.ds(0, half)], ssem.at[18])

    scale = 1.0 / math.sqrt(PATCH)
    extra = yfull[4 * ROWT : 5 * ROWT].reshape(NI, 128)
    main = jnp.zeros((256, FT), F32)
    small = jnp.zeros((256, FT), F32)
    for q in range(4):
        main = main + dot_nn(ept[q], yfull[q * ROWT : (q + 1) * ROWT].reshape(NI, 128))
        tail = dot_nn(ept[q], extra)
        small = small + (tail if q == 0 else pltpu.roll(tail, 128 - 8 * q, 1))
    fin[r, 0:208] = (main[0:208] * scale).astype(BF16)
    turned = (small * scale).T
    fin[r, 208:224] = jnp.concatenate([turned[0:8, 0:128], turned[0:8, 128:256]], axis=0).astype(BF16)

    send(fin.at[r], fin.at[r], 19, other_y)

    def ring(n, flow, step, sign):
        piece = fin.at[lax.rem(z + 12 - sign * step, 12) * 2 + flow]
        send(piece, piece, n, dev_z(1 if sign > 0 else 11))

    flows = (yh, 1 - yh)
    first = 20

    def number(f, step, way):
        return first + (f * 6 + step) * 2 + way

    def begin(f):
        ring(number(f, 0, 0), flows[f], 0, 1)
        ring(number(f, 0, 1), flows[f], 0, -1)

    def forward(f, step):
        for way in range(2):
            if step >= 6 - way:
                continue
            n = number(f, step, way)
            await_bytes(fin.at[0], rsem.at[n])
            if step + 1 < 6 - way:
                ring(number(f, step + 1, way), flows[f], step + 1, 1 - 2 * way)

    begin(0)
    for step in range(6 + LAG):
        if step == LAG:
            await_bytes(fin.at[0], rsem.at[19])
            await_bytes(fin.at[0], ssem.at[19])
            begin(1)
        if step < 6:
            forward(0, step)
        if step >= LAG:
            forward(1, step - LAG)

    for s in range(24):
        out[:, s * 128 : (s + 1) * 128] = fin[s, 0:EC]
    ends = [jnp.concatenate([fin[s, 208:216], fin[s, 216:224]], axis=1).astype(F32) for s in range(16)]
    out[:, 3072:3200] = jnp.concatenate(ends, axis=0).T[0:EC].astype(BF16)

    await_bytes(ra1, ssem.at[0])
    await_bytes(ra2, ssem.at[1])
    await_bytes(ra3, ssem.at[2])
    await_bytes(rb1, ssem.at[6])
    await_bytes(rb2, ssem.at[7])
    await_bytes(rc1, ssem.at[9])
    await_bytes(rc2, ssem.at[15])
    await_bytes(c2.at[pl.ds(0, 3)], ssem.at[16])
    for f in range(2):
        for step in range(6):
            for way in range(2):
                if way == 1 and step == 5:
                    continue
                await_bytes(fin.at[0], ssem.at[number(f, step, way)])


def shards(out_grad, gate_pre, up_pre, w_gate, w_up, w_down, w_proj, enc_hidden, route, img_count):
    any_spec = pl.BlockSpec(memory_space=pl.ANY)
    vmem = pltpu.VMEM
    tile = (16, 128)
    n_sem = 20 + 24
    result = pl.pallas_call(
        kernel,
        out_shape=jax.ShapeDtypeStruct((EC, 3200), BF16),
        in_specs=[any_spec] * 8
        + [pl.BlockSpec(memory_space=pltpu.VMEM), pl.BlockSpec(memory_space=pltpu.SMEM)],
        out_specs=pl.BlockSpec(memory_space=pltpu.VMEM),
        scratch_shapes=[
            vmem((NI, KD), BF16),
            vmem((HIDP, KD), BF16),
            vmem((HIDP, KD), BF16),
            vmem((HIDP, KD), BF16),
            vmem((544, KD), BF16),
            vmem((640, KD), BF16),
            vmem((GR, HID), BF16),
            vmem((GR, HID), BF16),
            vmem((48, EC), BF16),
            vmem((48, HIDP), BF16),
            vmem((48, HIDP), BF16),
            vmem((2, 4, 2, GRP, 640), BF16),
            vmem((24, 48, 256), BF16),
            vmem((HT, *tile), BF16),
            vmem((HT // 2, *tile), BF16),
            vmem((4, 24, *tile), BF16),
            vmem((3, 24, *tile), BF16),
            vmem((4, 6, *tile), BF16),
            vmem((3, 6, *tile), BF16),
            vmem((HT, *tile), BF16),
            vmem((LT, NI, 128), F32),
            vmem((LT, NI, 128), F32),
            vmem((72, 8, 128), BF16),
            vmem((11, 6, 8, 128), BF16),
            vmem((6, 8, 128), BF16),
            vmem((6, 8, 128), BF16),
            vmem((72, 8, 128), BF16),
            vmem((4, 256, NI), BF16),
            vmem((YT, *tile), BF16),
            vmem((YT // 2, *tile), BF16),
            vmem((4, 12, *tile), BF16),
            vmem((3, 12, *tile), BF16),
            vmem((4, 12, *tile), BF16),
            vmem((YT, *tile), BF16),
            vmem((24, PIECE, 128), BF16),
            pltpu.SemaphoreType.DMA((9,)),
            pltpu.SemaphoreType.DMA((n_sem,)),
            pltpu.SemaphoreType.DMA((n_sem,)),
        ],
        compiler_params=pltpu.CompilerParams(
            collective_id=0, has_side_effects=True, vmem_limit_bytes=56 * 1024 * 1024
        ),
    )(
        out_grad, gate_pre, up_pre, w_gate.T, w_up.T, w_down, w_proj, enc_hidden,
        route.reshape(1, NI), img_count,
    )
    return result.T


def solution(mesh):
    placed = (
        P(None, ("enc", "col")),
        P("enc", "row"),
        P("enc", "row"),
        P(("enc", "col"), "row"),
        P(("enc", "col"), "row"),
        P("row", ("enc", "col")),
        P(None, ("enc", "col")),
        P("row", ("enc", "col")),
        P(),
        P(),
    )
    return jax.shard_map(
        shards, mesh=mesh, in_specs=placed, out_specs=P(None, ("enc", "col")), check_vma=False
    )
```

time: 519 us -> 126 us (0.24)
  waiting for transfers between devices: 336 us -> 0 us
  blocking collectives: 135 us -> 0 us
  Pallas kernels: 0 us -> 120 us
  local copies, waits for them, and re-layouts: 18.2 us -> 3.68 us
  between operations: 13.6 us -> 0.01 us
  matrix products: 9.51 us -> 0 us
    psum x1 -> x0, waiting for transfers between devices: 295 us -> none  [shards(): total = lax.psum(group_term.astype(jnp.bfloat16), 'row')]
    pallas_call x0 -> x1, Pallas kernels: none -> 120 us  [shards(): pl.pallas_call(kernel, out_shape=jax.ShapeDtypeStruct((EC, 3200), BF16),...]
    all_to_all x4 -> x0, blocking collectives: 120 us -> none  [the longest x3 102 us: summed_on_arrival(): parts = lax.all_to_all(split_up(x, dim, size), axis, 0, 0, tiled=True)]
    all_gather x1 -> x0, waiting for transfers between devices: 29.7 us -> none  [sent_together(): lax.all_gather(both, axis, axis=dim, tiled=True)]
    all_gather x1 -> x0, blocking collectives: 14.7 us -> none  [sent_together(): lax.all_gather(both, axis, axis=dim, tiled=True)]
    all_to_all x1 -> x0, waiting for transfers between devices: 10.4 us -> none  [summed_on_arrival(): parts = lax.all_to_all(split_up(x, dim, size), axis, 0, 0, tiled=True)]
    dot_general x5 -> x0, matrix products: 9.51 us -> none  [the longest x4 7.91 us: contract_last(): lax.dot_general(left, right, (((1,), (1,)), ((), ())), preferred_element_...]
  transfers between devices with their start and end apart: 3 -> 0, of which waited for: 3 -> 0; matrix products, arithmetic and copies ran while one was open for 0% -> 0% of each run, Pallas kernels for 0% -> 0%
where the time goes in v1:
time: 126 us; the launch traced here: 124 us
  Pallas kernels  120 us (95%)
  local copies, waits for them, and re-layouts  3.68 us (3%)
    pallas_call x1, Pallas kernels, shards(): pl.pallas_call(kernel, out_shape=jax.ShapeDtypeStruct((EC, 3200), BF16),...  120 us

profile of v1, /device:TPU:6, one launch (start us, length us, event | category | flops | bytes accessed | tf_op | source)
XLA Modules:
  0.0 123.7 jit_solution(9786829734125581539)
XLA Ops:
  0.0 1.2 %reshape.3.rt = s32[1,288]{1,0:T(1,128)} reshape(s32[288]{0:T(512)} %param.18) | data formatting | bytes 2304 | tf_op jit(solution)/shard_map/reshape | solution.py:453
  1.2 120.1 %shard_map.100 = bf16[200,3200]{1,0:T(8,128)(2,1)} custom-call(bf16[288,256]{1,0:T(8,128)(2,1)} %og_h.1, bf16[36,1232]{1,0:T(8,128)(2,1)} %g_h.1, bf16[36,1232]{1,0:T(8,128)(2,1)} %u_h.1, bf16[1232,256]{1,0:T(8,128)(2,1)} %bitcast.4, bf16[1232,256]{1,0:T(8,128)(2,1)} %bitcast.5, bf16[1232,256]{1,0:T(8,128)(2,1)} %wd_h.1, bf16[12800,256]{1,0:T(8,128)(2,1)} %wp_h.1, ...), custom_call_target="tpu_custom_call" | custom-call | tf_op jit(solution)/shard_map/pallas_call | solution.py:402
  121.3 2.4 %copy.12 = bf16[3200,200]{0,1:T(8,128)(2,1)} copy(bf16[3200,200]{0,1:T(8,128)(2,1)} %bitcast.3) | data formatting | bytes 2560000

commit v2 on v1

--- a/solution.py
+++ b/solution.py
@@ -27,6 +27,7 @@
 PATCH = 1152
 FT = 128
 PIECE = 224
+CUT = PIECE // 2
 LAG = 2
 
 
@@ -53,7 +54,7 @@
 def kernel(
     og_h, g_h, u_h, wg_h, wu_h, wd_h, wp_h, eh_h, rt, cnt, out,
     og, wd, wg, wu, wpm, wpp, graw, uraw, eraw, gpad, upad,
-    gu, ebuf, hbuf, ra1, s1, ra2, s2, ra3, hfull, fa, fb,
+    gu, ebuf, hbuf, ra1, s1, s1b, ra2, s2, ra3, hfull, fa, fb,
     xb, rb1, sb, rb2, xfull, ept,
     yb, rc1, c1, rc2, c2, yfull, fin,
     lsem, ssem, rsem,
@@ -83,11 +84,57 @@
     def dev_z(k):
         return (e, at_z(k) * 2 + yh, c)
 
+    totals = {
+        0: ra1, 2: ra3, 3: hfull.at[pl.ds(0, 18)],
+        5: hfull.at[pl.ds(0, HT // 2)], 6: rb1, 7: rb2, 8: xfull.at[pl.ds(0, 66)], 9: rc1,
+        10: gu.at[:, 0, 0], 11: gu.at[:, 0, 0], 12: ebuf.at[0],
+        13: ebuf.at[pl.ds(0, 22)], 14: gu.at[:, :, 0], 15: rc2, 16: c2.at[pl.ds(0, 3)],
+        17: yfull.at[pl.ds(0, 36)], 18: yfull.at[pl.ds(0, YT // 2)],
+    }
+    for n in (21, 22):
+        totals[n] = gu.at[0, 0, 0]
+    for n in range(23, 29):
+        totals[n] = hfull.at[pl.ds(0, 12)]
+    for n in range(29, 31):
+        totals[n] = ra2.at[0, 0]
+    for n in range(31, 35):
+        totals[n] = ra2.at[0, 0]
+    unsent, unread = [], []
+
+    def arrived(n):
+        unread.remove(n)
+        await_bytes(totals.get(n, fin.at[0, pl.ds(0, CUT)]), rsem.at[n])
+
+    def left(n):
+        unsent.remove(n)
+        await_bytes(totals.get(n, fin.at[0, pl.ds(0, CUT)]), ssem.at[n])
+
     def send(src, dst, n, to):
+        if n not in unsent:
+            unsent.append(n)
+            unread.append(n)
         pltpu.make_async_remote_copy(
             src_ref=src, dst_ref=dst, send_sem=ssem.at[n], recv_sem=rsem.at[n],
             device_id=to, device_id_type=MESH,
         ).start()
+
+    def block(ref, base, size, k, h):
+        return ref.at[pl.ds(base + at_x(k) * size + h * (size // 2), size // 2)]
+
+    def gather_x(ref, base, size, n):
+        for k, h, m in ((1, 0, 0), (3, 1, 1), (1, 1, 2), (3, 0, 3)):
+            own = block(ref, base, size, 0, h)
+            send(own, own, n + m, dev_x(k))
+
+    def gathered_x(ref, base, size, n):
+        arrived(n)
+        far = block(ref, base, size, 3, 0)
+        send(far, far, n + 4, dev_x(1))
+        arrived(n + 1)
+        far = block(ref, base, size, 1, 1)
+        send(far, far, n + 5, dev_x(3))
+        for m in (2, 3, 4, 5):
+            arrived(n + m)
 
     def local(src, dst, n):
         copy = pltpu.make_async_copy(src, dst, lsem.at[n])
@@ -154,26 +201,31 @@
 
     half = HT // 2
     send(hbuf.at[pl.ds((1 - core) * half, half)], ra1, 0, sib)
-    for k in range(1, 4):
-        send(gu.at[0, x, core], gu.at[0, x, core], 10, dev_x(k))
     send(ebuf.at[r], ebuf.at[r], 12, other_y)
-    await_bytes(ra1, rsem.at[0])
+    arrived(0)
     mine = hbuf[pl.ds(core * half, half)].astype(F32) + ra1[...].astype(F32)
-    s1[...] = mine.astype(BF16).reshape(4, 24, 16, 128)
-
-    for k in range(1, 4):
-        send(s1.at[at_x(k)], ra2.at[k - 1], 1, dev_x(k))
-    for k in range(1, 4):
-        send(gu.at[1, x, core], gu.at[1, x, core], 11, dev_x(k))
-    await_bytes(ebuf.at[0], rsem.at[12])
-    await_bytes(ebuf.at[0], ssem.at[12])
+    s1[...] = mine.astype(BF16).reshape(4, 2, 12, 16, 128)
+
+    near, far, back = at_x(1), at_x(2), at_x(3)
+    send(s1.at[far, 0], ra2.at[0, 0], 29, dev_x(1))
+    send(s1.at[far, 1], ra2.at[0, 1], 30, dev_x(3))
+    send(s1.at[near, 1], ra2.at[1, 1], 31, dev_x(1))
+    send(s1.at[back, 0], ra2.at[2, 0], 32, dev_x(3))
+    arrived(29)
+    s1b[0] = (s1[near, 0].astype(F32) + ra2[0, 0].astype(F32)).astype(BF16)
+    send(s1b.at[0], ra2.at[1, 0], 33, dev_x(1))
+    arrived(30)
+    s1b[1] = (s1[back, 1].astype(F32) + ra2[0, 1].astype(F32)).astype(BF16)
+    send(s1b.at[1], ra2.at[2, 1], 34, dev_x(3))
+    send(gu.at[:, x, core], gu.at[:, x, core], 10, dev_x(1))
+    send(gu.at[:, x, core], gu.at[:, x, core], 11, dev_x(3))
+    arrived(12)
     pair = ebuf.at[pl.ds(2 * z, 2)]
     for k in range(1, 12):
         send(pair, pair, 13, dev_z(k))
-    await_bytes(ra2, rsem.at[1])
-    got = s1[x].astype(F32)
-    for k in range(3):
-        got = got + ra2[k].astype(F32)
+    for n in (31, 32, 33, 34):
+        arrived(n)
+    got = s1[x].astype(F32) + ra2[1].astype(F32) + ra2[2].astype(F32)
     s2[...] = got.astype(BF16).reshape(4, 6, 16, 128)
 
     for k in range(1, 4):
@@ -188,7 +240,7 @@
     move = onehot((lane == 4 * (row & 7) + (row >> 3)) & (row < 32))
     wpp[512:640, :] = dot_nn(move, wpm[512:544, :]).astype(BF16)
 
-    await_bytes(ra3, rsem.at[2])
+    arrived(2)
     got = s2[c].astype(F32)
     for k in range(3):
         got = got + ra3[k].astype(F32)
@@ -198,19 +250,17 @@
     own = hfull.at[pl.ds(base + c * 6, 6)]
     for k in range(1, 4):
         send(own, own, 3, dev_c(k))
-    await_bytes(gu.at[0, pl.ds(0, 3), 0], rsem.at[10])
-    await_bytes(gu.at[0, pl.ds(0, 3), 0], rsem.at[11])
-    await_bytes(gu.at[0, pl.ds(0, 3), 0], ssem.at[10])
-    await_bytes(gu.at[0, pl.ds(0, 3), 0], ssem.at[11])
+    arrived(10)
+    send(gu.at[0, at_x(3), core], gu.at[0, at_x(3), core], 21, dev_x(1))
+    arrived(11)
+    send(gu.at[1, at_x(1), core], gu.at[1, at_x(1), core], 22, dev_x(3))
+    arrived(3)
+    gather_x(hfull, core * half, 24, 23)
+    arrived(21)
+    arrived(22)
     send(gu.at[:, :, core], gu.at[:, :, core], 14, sib)
-    await_bytes(hfull.at[pl.ds(0, 18)], rsem.at[3])
-    await_bytes(hfull.at[pl.ds(0, 18)], ssem.at[3])
-    own = hfull.at[pl.ds(base, 24)]
-    for k in range(1, 4):
-        send(own, own, 4, dev_x(k))
-
-    await_bytes(gu.at[:, :, 0], rsem.at[14])
-    await_bytes(gu.at[:, :, 0], ssem.at[14])
+
+    arrived(14)
     col = iota((NI, 8 * GRP), 1)
     target = col
     for s in range(1, 8):
@@ -236,14 +286,12 @@
 
         lax.fori_loop(0, 5, factors, 0)
 
-    await_bytes(hfull.at[pl.ds(0, 72)], rsem.at[4])
-    await_bytes(hfull.at[pl.ds(0, 72)], ssem.at[4])
+    gathered_x(hfull, core * half, 24, 23)
     own = hfull.at[pl.ds(core * half, half)]
     send(own, own, 5, sib)
     load_wg.wait()
     load_wu.wait()
-    await_bytes(hfull.at[pl.ds(0, half)], rsem.at[5])
-    await_bytes(hfull.at[pl.ds(0, half)], ssem.at[5])
+    arrived(5)
 
     def inputs(j, total):
         h = hfull[pl.ds(j * ROWT, ROWT)].astype(F32).reshape(NI, 128)
@@ -258,14 +306,13 @@
     for k in range(1, 12):
         send(xb.at[pl.ds(at_z(k) * 6, 6)], rb1.at[k - 1], 6, dev_z(k))
 
-    await_bytes(ebuf.at[pl.ds(0, 22)], rsem.at[13])
-    await_bytes(ebuf.at[pl.ds(0, 22)], ssem.at[13])
+    arrived(13)
     lane = iota((1, NI), 1)
     limit = jnp.zeros((1, NI), jnp.int32)
     for s in range(24):
         inside = (lane >= s * IMG) & (lane < (s + 1) * IMG)
         limit = jnp.where(inside, s * IMG + cnt[s], limit)
-    slot_row = jnp.where(lane < limit, rt[...], -1)
+    slot_row = jnp.where(lane < limit, rt[...].reshape(1, NI), -1)
     routed = onehot(iota((NI, NI), 0) == slot_row)
     et = ebuf[...].reshape(PATCH, 256).astype(F32).T.astype(BF16)
     for q in range(4):
@@ -273,43 +320,42 @@
         plane = dot_nn(et, take).astype(BF16)
         ept[q] = dot_nt(plane, routed).astype(BF16)
 
-    await_bytes(rb1, rsem.at[6])
+    arrived(6)
     got = xb[pl.ds(z * 6, 6)].astype(F32)
     for k in range(11):
         got = got + rb1[k].astype(F32)
     sb[...] = got.astype(BF16)
     send(sb, rb2, 7, other_y)
-    await_bytes(rb2, rsem.at[7])
+    arrived(7)
     xfull[pl.ds(z * 6, 6)] = (sb[...].astype(F32) + rb2[...].astype(F32)).astype(BF16)
     own = xfull.at[pl.ds(z * 6, 6)]
     for k in range(1, 12):
         send(own, own, 8, dev_z(k))
-    await_bytes(xfull.at[pl.ds(0, 66)], rsem.at[8])
-    await_bytes(xfull.at[pl.ds(0, 66)], ssem.at[8])
+    arrived(8)
 
     both = xfull[...].astype(F32)
-    left = both[0:36].reshape(NI, 128).astype(BF16)
-    right = both[36:72].reshape(NI, 128).astype(BF16)
+    low = both[0:36].reshape(NI, 128).astype(BF16)
+    high = both[36:72].reshape(NI, 128).astype(BF16)
     for q in range(5):
         w = wpp[q * 128 : (q + 1) * 128, :]
-        part = dot_nt(left, w[:, 0:128]) + dot_nt(right, w[:, 128:256])
+        part = dot_nt(low, w[:, 0:128]) + dot_nt(high, w[:, 128:256])
         yb[q * ROWT : (q + 1) * ROWT] = part.reshape(ROWT, 16, 128).astype(BF16)
 
     half = YT // 2
     send(yb.at[pl.ds((1 - core) * half, half)], rc1, 9, sib)
-    await_bytes(rc1, rsem.at[9])
+    arrived(9)
     mine = yb[pl.ds(core * half, half)].astype(F32) + rc1[...].astype(F32)
     c1[...] = mine.astype(BF16).reshape(4, 12, 16, 128)
     for k in range(1, 4):
         send(c1.at[at_x(k)], rc2.at[k - 1], 15, dev_x(k))
-    await_bytes(rc2, rsem.at[15])
+    arrived(15)
     got = c1[x].astype(F32)
     for k in range(3):
         got = got + rc2[k].astype(F32)
     c2[c] = got.astype(BF16)
     for k in range(1, 4):
         send(c2.at[c], c2.at[c], 16, dev_c(k))
-    await_bytes(c2.at[pl.ds(0, 3)], rsem.at[16])
+    arrived(16)
     got = c2[0].astype(F32)
     for k in range(1, 4):
         got = got + c2[k].astype(F32)
@@ -318,12 +364,10 @@
     own = yfull.at[pl.ds(base, 12)]
     for k in range(1, 4):
         send(own, own, 17, dev_x(k))
-    await_bytes(yfull.at[pl.ds(0, 36)], rsem.at[17])
-    await_bytes(yfull.at[pl.ds(0, 36)], ssem.at[17])
+    arrived(17)
     own = yfull.at[pl.ds(core * half, half)]
     send(own, own, 18, sib)
-    await_bytes(yfull.at[pl.ds(0, half)], rsem.at[18])
-    await_bytes(yfull.at[pl.ds(0, half)], ssem.at[18])
+    arrived(18)
 
     scale = 1.0 / math.sqrt(PATCH)
     extra = yfull[4 * ROWT : 5 * ROWT].reshape(NI, 128)
@@ -337,68 +381,74 @@
     turned = (small * scale).T
     fin[r, 208:224] = jnp.concatenate([turned[0:8, 0:128], turned[0:8, 128:256]], axis=0).astype(BF16)
 
-    send(fin.at[r], fin.at[r], 19, other_y)
-
-    def ring(n, flow, step, sign):
-        piece = fin.at[lax.rem(z + 12 - sign * step, 12) * 2 + flow]
-        send(piece, piece, n, dev_z(1 if sign > 0 else 11))
+    def part_of(slot, h):
+        return fin.at[slot, pl.ds(h * CUT, CUT)]
+
+    for h in range(2):
+        send(part_of(r, h), part_of(r, h), 19 + h, other_y)
 
     flows = (yh, 1 - yh)
-    first = 20
-
-    def number(f, step, way):
-        return first + (f * 6 + step) * 2 + way
-
-    def begin(f):
-        ring(number(f, 0, 0), flows[f], 0, 1)
-        ring(number(f, 0, 1), flows[f], 0, -1)
-
-    def forward(f, step):
+
+    def hops(h, way):
+        return 6 if h == way else 5
+
+    def number(f, h, step, way):
+        return 37 + ((f * 2 + h) * 6 + step) * 2 + way
+
+    def slot_at(f, step, way):
+        behind = 12 - step if way == 0 else step
+        return lax.rem(z + behind, 12) * 2 + flows[f]
+
+    def ring(f, h, step, way):
+        piece = part_of(slot_at(f, step, way), h)
+        send(piece, piece, number(f, h, step, way), dev_z(1 if way == 0 else 11))
+
+    def place(slot, h):
+        lanes = pl.ds(pl.multiple_of(slot * 128, 128), 128)
+        low, top = (0, CUT) if h == 0 else (CUT, EC)
+        out[low:top, lanes] = fin[slot, low:top]
+
+    def begin(f, h):
         for way in range(2):
-            if step >= 6 - way:
-                continue
-            n = number(f, step, way)
-            await_bytes(fin.at[0], rsem.at[n])
-            if step + 1 < 6 - way:
-                ring(number(f, step + 1, way), flows[f], step + 1, 1 - 2 * way)
-
-    begin(0)
-    for step in range(6 + LAG):
-        if step == LAG:
-            await_bytes(fin.at[0], rsem.at[19])
-            await_bytes(fin.at[0], ssem.at[19])
-            begin(1)
-        if step < 6:
-            forward(0, step)
-        if step >= LAG:
-            forward(1, step - LAG)
-
-    for s in range(24):
-        out[:, s * 128 : (s + 1) * 128] = fin[s, 0:EC]
+            ring(f, h, 0, way)
+        place(slot_at(f, 0, 0), h)
+
+    def forward(f, h, step):
+        for way in range(2):
+            if step < hops(h, way):
+                arrived(number(f, h, step, way))
+                if step + 1 < hops(h, way):
+                    ring(f, h, step + 1, way)
+        for way in range(2):
+            if step < hops(h, way):
+                place(slot_at(f, step + 1, way), h)
+
+    begin(0, 0)
+    begin(0, 1)
+    for tick in range(6 + LAG + 1):
+        for h in range(2):
+            if tick == LAG + h:
+                arrived(19 + h)
+                begin(1, h)
+        for h in range(2):
+            if tick < 6:
+                forward(0, h, tick)
+        for h in range(2):
+            if 0 <= tick - LAG - h < 6:
+                forward(1, h, tick - LAG - h)
+
     ends = [jnp.concatenate([fin[s, 208:216], fin[s, 216:224]], axis=1).astype(F32) for s in range(16)]
     out[:, 3072:3200] = jnp.concatenate(ends, axis=0).T[0:EC].astype(BF16)
 
-    await_bytes(ra1, ssem.at[0])
-    await_bytes(ra2, ssem.at[1])
-    await_bytes(ra3, ssem.at[2])
-    await_bytes(rb1, ssem.at[6])
-    await_bytes(rb2, ssem.at[7])
-    await_bytes(rc1, ssem.at[9])
-    await_bytes(rc2, ssem.at[15])
-    await_bytes(c2.at[pl.ds(0, 3)], ssem.at[16])
-    for f in range(2):
-        for step in range(6):
-            for way in range(2):
-                if way == 1 and step == 5:
-                    continue
-                await_bytes(fin.at[0], ssem.at[number(f, step, way)])
+    for n in list(unsent):
+        left(n)
 
 
 def shards(out_grad, gate_pre, up_pre, w_gate, w_up, w_down, w_proj, enc_hidden, route, img_count):
     any_spec = pl.BlockSpec(memory_space=pl.ANY)
     vmem = pltpu.VMEM
     tile = (16, 128)
-    n_sem = 20 + 24
+    n_sem = 37 + 48
     result = pl.pallas_call(
         kernel,
         out_shape=jax.ShapeDtypeStruct((EC, 3200), BF16),
@@ -421,8 +471,9 @@
             vmem((24, 48, 256), BF16),
             vmem((HT, *tile), BF16),
             vmem((HT // 2, *tile), BF16),
-            vmem((4, 24, *tile), BF16),
-            vmem((3, 24, *tile), BF16),
+            vmem((4, 2, 12, *tile), BF16),
+            vmem((2, 12, *tile), BF16),
+            vmem((3, 2, 12, *tile), BF16),
             vmem((4, 6, *tile), BF16),
             vmem((3, 6, *tile), BF16),
             vmem((HT, *tile), BF16),
@@ -450,7 +501,7 @@
         ),
     )(
         out_grad, gate_pre, up_pre, w_gate.T, w_up.T, w_down, w_proj, enc_hidden,
-        route.reshape(1, NI), img_count,
+        route, img_count,
     )
     return result.T
 

time: 126 us -> 125 us (level)
  no operation moved by 1% of the time
where the time goes in v2:
time: 125 us; the launch traced here: 123 us
  Pallas kernels  120 us (96%)
  local copies, waits for them, and re-layouts  2.44 us (2%)
    pallas_call x1, Pallas kernels, shards(): pl.pallas_call(kernel, out_shape=jax.ShapeDtypeStruct((EC, 3200), BF16),...  120 us

profile of v2, /device:TPU:6, one launch (start us, length us, event | category | flops | bytes accessed | tf_op | source)
XLA Modules:
  0.0 122.7 jit_solution(8469766431920694955)
XLA Ops:
  0.0 120.2 %shard_map.100 = bf16[200,3200]{1,0:T(8,128)(2,1)} custom-call(bf16[288,256]{1,0:T(8,128)(2,1)} %og_h.1, bf16[36,1232]{1,0:T(8,128)(2,1)} %g_h.1, bf16[36,1232]{1,0:T(8,128)(2,1)} %u_h.1, bf16[1232,256]{1,0:T(8,128)(2,1)} %bitcast.4, bf16[1232,256]{1,0:T(8,128)(2,1)} %bitcast.5, bf16[1232,256]{1,0:T(8,128)(2,1)} %wd_h.1, bf16[12800,256]{1,0:T(8,128)(2,1)} %wp_h.1, ...), custom_call_target="tpu_custom_call" | custom-call | tf_op jit(solution)/shard_map/pallas_call | solution.py:452
  120.2 2.4 %copy.12 = bf16[3200,200]{0,1:T(8,128)(2,1)} copy(bf16[3200,200]{0,1:T(8,128)(2,1)} %bitcast.3) | data formatting | bytes 2560000

commit v3 on v2

--- a/solution.py
+++ b/solution.py
@@ -28,7 +28,7 @@
 FT = 128
 PIECE = 224
 CUT = PIECE // 2
-LAG = 2
+LAG = 1
 
 
 def dot_nt(a, b):
@@ -395,13 +395,16 @@
     def number(f, h, step, way):
         return 37 + ((f * 2 + h) * 6 + step) * 2 + way
 
-    def slot_at(f, step, way):
-        behind = 12 - step if way == 0 else step
+    def slot_at(f, away, way):
+        behind = 12 - away if way == 0 else away
         return lax.rem(z + behind, 12) * 2 + flows[f]
 
-    def ring(f, h, step, way):
-        piece = part_of(slot_at(f, step, way), h)
-        send(piece, piece, number(f, h, step, way), dev_z(1 if way == 0 else 11))
+    def ring(f, h, away, way):
+        piece = part_of(slot_at(f, away, way), h)
+        for jump in (2, 1):
+            if away + jump <= hops(h, way):
+                to = dev_z(jump if way == 0 else 12 - jump)
+                send(piece, piece, number(f, h, away + jump - 1, way), to)
 
     def place(slot, h):
         lanes = pl.ds(pl.multiple_of(slot * 128, 128), 128)
@@ -413,29 +416,30 @@
             ring(f, h, 0, way)
         place(slot_at(f, 0, 0), h)
 
-    def forward(f, h, step):
-        for way in range(2):
-            if step < hops(h, way):
-                arrived(number(f, h, step, way))
-                if step + 1 < hops(h, way):
-                    ring(f, h, step + 1, way)
-        for way in range(2):
-            if step < hops(h, way):
-                place(slot_at(f, step + 1, way), h)
+    def forward(f, h, tick):
+        for away in (2 * tick + 2, 2 * tick + 1):
+            for way in range(2):
+                if away <= hops(h, way):
+                    arrived(number(f, h, away - 1, way))
+                    if away % 2 == 0:
+                        ring(f, h, away, way)
+            for way in range(2):
+                if away <= hops(h, way):
+                    place(slot_at(f, away, way), h)
 
     begin(0, 0)
     begin(0, 1)
-    for tick in range(6 + LAG + 1):
-        for h in range(2):
-            if tick == LAG + h:
+    for tick in range(3 + LAG):
+        if tick == LAG:
+            for h in range(2):
                 arrived(19 + h)
                 begin(1, h)
         for h in range(2):
-            if tick < 6:
+            if tick < 3:
                 forward(0, h, tick)
         for h in range(2):
-            if 0 <= tick - LAG - h < 6:
-                forward(1, h, tick - LAG - h)
+            if tick >= LAG:
+                forward(1, h, tick - LAG)
 
     ends = [jnp.concatenate([fin[s, 208:216], fin[s, 216:224]], axis=1).astype(F32) for s in range(16)]
     out[:, 3072:3200] = jnp.concatenate(ends, axis=0).T[0:EC].astype(BF16)
@@ -445,7 +449,7 @@
 
 
 def shards(out_grad, gate_pre, up_pre, w_gate, w_up, w_down, w_proj, enc_hidden, route, img_count):
-    any_spec = pl.BlockSpec(memory_space=pl.ANY)
+    any_spec = pl.BlockSpec(memory_space=pltpu.HBM)
     vmem = pltpu.VMEM
     tile = (16, 128)
     n_sem = 37 + 48

time: 125 us -> 118 us (0.944)
  the two profiles are of different devices: /device:TPU:6 before, /device:TPU:1 now
where the time goes in v3:
time: 118 us
  Pallas kernels  116 us (98%)
  local copies, waits for them, and re-layouts  2.44 us (2%)
    pallas_call x1, Pallas kernels, shards(): pl.pallas_call(kernel, out_shape=jax.ShapeDtypeStruct((EC, 3200), BF16),...  116 us
    unnamed x1, local copies, waits for them, and re-layouts  2.44 us

profile of v3, /device:TPU:1, one launch (start us, length us, event | category | flops | bytes accessed | tf_op | source)
XLA Modules:
  0.0 118.2 jit_solution(14436213217032325275)
XLA Ops:
  0.0 115.7 %shard_map.100 = bf16[200,3200]{1,0:T(8,128)(2,1)} custom-call(bf16[288,256]{1,0:T(8,128)(2,1)} %og_h.1, bf16[36,1232]{1,0:T(8,128)(2,1)} %g_h.1, bf16[36,1232]{1,0:T(8,128)(2,1)} %u_h.1, bf16[1232,256]{1,0:T(8,128)(2,1)} %bitcast.4, bf16[1232,256]{1,0:T(8,128)(2,1)} %bitcast.5, bf16[1232,256]{1,0:T(8,128)(2,1)} %wd_h.1, bf16[12800,256]{1,0:T(8,128)(2,1)} %wp_h.1, ...), custom_call_target="tpu_custom_call" | custom-call | tf_op jit(solution)/shard_map/pallas_call | solution.py:456
  115.7 2.4 %copy.12 = bf16[3200,200]{0,1:T(8,128)(2,1)} copy(bf16[3200,200]{0,1:T(8,128)(2,1)} %bitcast.3) | data formatting | bytes 2560000

commit v4 on v3

--- a/solution.py
+++ b/solution.py
@@ -28,7 +28,6 @@
 FT = 128
 PIECE = 224
 CUT = PIECE // 2
-LAG = 1
 
 
 def dot_nt(a, b):
@@ -56,7 +55,7 @@
     og, wd, wg, wu, wpm, wpp, graw, uraw, eraw, gpad, upad,
     gu, ebuf, hbuf, ra1, s1, s1b, ra2, s2, ra3, hfull, fa, fb,
     xb, rb1, sb, rb2, xfull, ept,
-    yb, rc1, c1, rc2, c2, yfull, fin,
+    yb, rc1, c1, rc2, c2, yfull, fin, last,
     lsem, ssem, rsem,
 ):
     e, r, c = lax.axis_index("enc"), lax.axis_index("row"), lax.axis_index("col")
@@ -126,15 +125,13 @@
             own = block(ref, base, size, 0, h)
             send(own, own, n + m, dev_x(k))
 
-    def gathered_x(ref, base, size, n):
+    def relay_x(ref, base, size, n):
         arrived(n)
         far = block(ref, base, size, 3, 0)
         send(far, far, n + 4, dev_x(1))
         arrived(n + 1)
         far = block(ref, base, size, 1, 1)
         send(far, far, n + 5, dev_x(3))
-        for m in (2, 3, 4, 5):
-            arrived(n + m)
 
     def local(src, dst, n):
         copy = pltpu.make_async_copy(src, dst, lsem.at[n])
@@ -259,6 +256,7 @@
     arrived(21)
     arrived(22)
     send(gu.at[:, :, core], gu.at[:, :, core], 14, sib)
+    relay_x(hfull, core * half, 24, 23)
 
     arrived(14)
     col = iota((NI, 8 * GRP), 1)
@@ -286,7 +284,8 @@
 
         lax.fori_loop(0, 5, factors, 0)
 
-    gathered_x(hfull, core * half, 24, 23)
+    for n in (25, 26, 27, 28):
+        arrived(n)
     own = hfull.at[pl.ds(core * half, half)]
     send(own, own, 5, sib)
     load_wg.wait()
@@ -399,9 +398,12 @@
         behind = 12 - away if way == 0 else away
         return lax.rem(z + behind, 12) * 2 + flows[f]
 
+    def jumps(f, away):
+        return (1,) if f == 0 else ((2, 1) if away % 2 == 0 else ())
+
     def ring(f, h, away, way):
         piece = part_of(slot_at(f, away, way), h)
-        for jump in (2, 1):
+        for jump in jumps(f, away):
             if away + jump <= hops(h, way):
                 to = dev_z(jump if way == 0 else 12 - jump)
                 send(piece, piece, number(f, h, away + jump - 1, way), to)
@@ -409,40 +411,39 @@
     def place(slot, h):
         lanes = pl.ds(pl.multiple_of(slot * 128, 128), 128)
         low, top = (0, CUT) if h == 0 else (CUT, EC)
-        out[low:top, lanes] = fin[slot, low:top]
+        pltpu.make_async_copy(
+            fin.at[slot, pl.ds(low, top - low)], out.at[pl.ds(low, top - low), lanes], lsem.at[9]
+        ).start()
 
     def begin(f, h):
         for way in range(2):
             ring(f, h, 0, way)
         place(slot_at(f, 0, 0), h)
 
-    def forward(f, h, tick):
-        for away in (2 * tick + 2, 2 * tick + 1):
-            for way in range(2):
-                if away <= hops(h, way):
-                    arrived(number(f, h, away - 1, way))
-                    if away % 2 == 0:
-                        ring(f, h, away, way)
-            for way in range(2):
-                if away <= hops(h, way):
-                    place(slot_at(f, away, way), h)
+    def forward(f, h, away):
+        for way in range(2):
+            if away <= hops(h, way):
+                arrived(number(f, h, away - 1, way))
+                ring(f, h, away, way)
+        for way in range(2):
+            if away <= hops(h, way):
+                place(slot_at(f, away, way), h)
 
     begin(0, 0)
     begin(0, 1)
-    for tick in range(3 + LAG):
-        if tick == LAG:
-            for h in range(2):
+    order = ((0, 1), (0, 2), (1, 0), (0, 3), (1, 2), (1, 1), (0, 4), (1, 4), (0, 5), (1, 3), (0, 6), (1, 6), (1, 5))
+    for f, away in order:
+        for h in range(2):
+            if away == 0:
                 arrived(19 + h)
-                begin(1, h)
-        for h in range(2):
-            if tick < 3:
-                forward(0, h, tick)
-        for h in range(2):
-            if tick >= LAG:
-                forward(1, h, tick - LAG)
+                begin(f, h)
+            else:
+                forward(f, h, away)
 
     ends = [jnp.concatenate([fin[s, 208:216], fin[s, 216:224]], axis=1).astype(F32) for s in range(16)]
-    out[:, 3072:3200] = jnp.concatenate(ends, axis=0).T[0:EC].astype(BF16)
+    last[...] = jnp.concatenate(ends, axis=0).T[0:EC].astype(BF16)
+    local(last, out.at[:, pl.ds(3072, 128)], 10).wait()
+    await_bytes(out.at[:, pl.ds(0, 3072)], lsem.at[9])
 
     for n in list(unsent):
         left(n)
@@ -458,7 +459,7 @@
         out_shape=jax.ShapeDtypeStruct((EC, 3200), BF16),
         in_specs=[any_spec] * 8
         + [pl.BlockSpec(memory_space=pltpu.VMEM), pl.BlockSpec(memory_space=pltpu.SMEM)],
-        out_specs=pl.BlockSpec(memory_space=pltpu.VMEM),
+        out_specs=any_spec,
         scratch_shapes=[
             vmem((NI, KD), BF16),
             vmem((HIDP, KD), BF16),
@@ -496,7 +497,8 @@
             vmem((4, 12, *tile), BF16),
             vmem((YT, *tile), BF16),
             vmem((24, PIECE, 128), BF16),
-            pltpu.SemaphoreType.DMA((9,)),
+            vmem((EC, 128), BF16),
+            pltpu.SemaphoreType.DMA((11,)),
             pltpu.SemaphoreType.DMA((n_sem,)),
             pltpu.SemaphoreType.DMA((n_sem,)),
         ],

time: 118 us -> 116 us (0.983)
  the two profiles are of different devices: /device:TPU:1 before, /device:TPU:6 now
where the time goes in v4:
time: 116 us; the launch traced here: 114 us
  Pallas kernels  112 us (97%)
  local copies, waits for them, and re-layouts  2.44 us (2%)
    pallas_call x1, Pallas kernels, shards(): pl.pallas_call(kernel, out_shape=jax.ShapeDtypeStruct((EC, 3200), BF16),...  112 us
    unnamed x1, local copies, waits for them, and re-layouts  2.44 us

profile of v4, /device:TPU:6, one launch (start us, length us, event | category | flops | bytes accessed | tf_op | source)
XLA Modules:
  0.0 114.3 jit_solution(15478547161979309126)
XLA Ops:
  0.0 111.8 %shard_map.100 = bf16[200,3200]{1,0:T(8,128)(2,1)} custom-call(bf16[288,256]{1,0:T(8,128)(2,1)} %og_h.1, bf16[36,1232]{1,0:T(8,128)(2,1)} %g_h.1, bf16[36,1232]{1,0:T(8,128)(2,1)} %u_h.1, bf16[1232,256]{1,0:T(8,128)(2,1)} %bitcast.4, bf16[1232,256]{1,0:T(8,128)(2,1)} %bitcast.5, bf16[1232,256]{1,0:T(8,128)(2,1)} %wd_h.1, bf16[12800,256]{1,0:T(8,128)(2,1)} %wp_h.1, ...), custom_call_target="tpu_custom_call" | custom-call | tf_op jit(solution)/shard_map/pallas_call | solution.py:457
  111.8 2.4 %copy.12 = bf16[3200,200]{0,1:T(8,128)(2,1)} copy(bf16[3200,200]{0,1:T(8,128)(2,1)} %bitcast.3) | data formatting | bytes 2560000
